TPU v7x, 32 devices: a whole 2x2x4 slice. The times are simulated.
32 devices in a mesh: attn: 4 (over y, x), expert: 8 (over z, core).
Axes of the slice: x: 2, y: 2, z: 4, core: 2. Of those that a mesh axis runs over, the one named last changes fastest.
Arguments:
- tokens: bfloat16 [1024, 2880], P(('attn', 'expert')), may hold values from -6 to 6
- expert_ids: int32 [1024, 4], P(('attn', 'expert')), may hold values from 0 to 7, all different within a row; in each aligned block of 32 rows (0 to 31, 32 to 63, ...) at most 32 rows name the same one
- gate_probs: float32 [1024, 4], P(('attn', 'expert')), may hold values from 0.05 to 0.6
- shed_blocks: int32 [8], replicated, may hold values from 0 to 4, as said below
- partner: int32 [8], replicated, may hold values from 0 to 7, as said below
- gate_weight: bfloat16 [8, 2880, 2880], P('expert', None, 'attn'), may hold values from -0.109375 to 0.109375
- up_weight: bfloat16 [8, 2880, 2880], P('expert', None, 'attn'), may hold values from -0.109375 to 0.109375
- down_weight: bfloat16 [8, 2880, 2880], P('expert', 'attn'), may hold values from -0.109375 to 0.109375
Outputs:
- moe_out: bfloat16 [1024, 2880], P(('attn', 'expert'))
Inputs may be any that keep to these rules, and one draw needn't show every extreme that they name: `expert_ids`: in the rows of one device, no expert is named by more than 32 rows; the 4 experts of a token differ. `shed_blocks`: some expert has exactly 4. partner pairs the experts: partner[partner[e]] = e and partner[e] != e.
All inputs are finite; a program needn't handle non-finite values.
Results may differ from a plain program's by a relative error of at most 0.0081.
Values may be sent and summed in bfloat16 or wider, within the bound.
A program may use at most 128 MiB of HBM per device.

v0:
```python
import jax
import jax.numpy as jnp
from jax import lax
from jax.sharding import PartitionSpec as P

SHED_MOST = 4
SWISH_SCALE = 1.702


def lookup(table, indices):
    places = jnp.arange(table.shape[0], dtype=jnp.int32)
    return jnp.sum(jnp.where(indices[:, None] == places[None, :], table[None, :], 0), axis=1)


def row_weights(all_ids, all_probs, shed_blocks, partner, capacity, block_size):
    me = lax.axis_index("expert").astype(jnp.int32)
    named = all_ids == me
    mask = jnp.any(named, axis=1).astype(jnp.int32)
    rank = jnp.cumsum(mask) - mask
    other = lookup(partner, me[None])
    bound = (
        capacity
        - block_size * lookup(shed_blocks, other)
        + block_size * lookup(shed_blocks, me[None])
    )
    weight = jnp.sum(jnp.where(named, all_probs, 0.0), axis=1)
    return jnp.where(rank < bound, weight, 0.0)


def on_device(
    tokens, expert_ids, gate_probs, shed_blocks, partner, gate_weight, up_weight, down_weight
):
    tok_rows, model_width = tokens.shape
    top_count = expert_ids.shape[1]
    capacity = tok_rows * top_count * lax.axis_size("attn")
    block_size = capacity // 8
    both = ("attn", "expert")
    all_ids = lax.all_gather(expert_ids, both, axis=0, tiled=True)
    all_probs = lax.all_gather(gate_probs, both, axis=0, tiled=True)
    rows = lax.all_gather(tokens, both, axis=0, tiled=True)
    weight = row_weights(all_ids, all_probs, shed_blocks, partner, capacity, block_size)
    gate_part = jnp.dot(rows, gate_weight[0], preferred_element_type=jnp.float32)
    up_part = jnp.dot(rows, up_weight[0], preferred_element_type=jnp.float32)
    hidden = gate_part * jax.nn.sigmoid(SWISH_SCALE * gate_part) * (up_part + 1.0)
    hidden = (hidden * weight[:, None]).astype(jnp.bfloat16)
    share = jnp.dot(hidden, down_weight[0], preferred_element_type=jnp.float32).astype(jnp.bfloat16)
    share = lax.psum_scatter(share, "attn", scatter_dimension=0, tiled=True)
    return lax.psum_scatter(share, "expert", scatter_dimension=0, tiled=True)


def solution(mesh):
    in_specs = (
        P(("attn", "expert"), None),
        P(("attn", "expert"), None),
        P(("attn", "expert"), None),
        P(),
        P(),
        P("expert", None, "attn"),
        P("expert", None, "attn"),
        P("expert", "attn", None),
    )
    out_specs = P(("attn", "expert"), None)
    return jax.shard_map(
        on_device, mesh=mesh, in_specs=in_specs, out_specs=out_specs, check_vma=False
    )
```

profile of v0, /device:TPU:0, one launch (start us, length us, event | category | flops | bytes accessed | tf_op | source)
XLA Modules:
  0.0 226.7 jit_solution(15309892988968563415)
XLA Ops:
  6.5 0.0 all-gather.4.cloned.1.call-start
  6.5 0.7 all-gather.4.cloned.1.call-update
  7.3 0.0 reduce-scatter.5.cloned.1.call-start
  7.3 44.1 %all-gather = s32[32,32,4]{1,2,0:T(4,128)S(1)} all-gather(s32[1,32,4]{1,2,0:T(4,128)} %bitcast.24), channel_id=1, replica_groups=mesh['attn'=4,'expert'=8] {'attn','expert'}, dimensions={0}, use_global_device_ids=true | all-gather | bytes 16896 | tf_op jit(solution)/shard_map/all_gather | solution.py:38
  51.4 0.1 fusion.19
  51.4 0.1 reshape.58
  51.5 0.1 reshape.68
  51.6 1.3 fusion.14
  52.9 2.0 fusion.15
  56.1 0.3 reduce-window.9
  56.4 0.1 slice.7
  56.5 37.9 %all-gather.1 = f32[32,32,4]{1,2,0:T(4,128)S(1)} all-gather(f32[1,32,4]{1,2,0:T(4,128)} %bitcast.25), channel_id=1, replica_groups=mesh['attn'=4,'expert'=8] {'attn','expert'}, dimensions={0}, use_global_device_ids=true | all-gather | bytes 16896 | tf_op jit(solution)/shard_map/all_gather | solution.py:39
  94.4 0.1 select_reduce_fusion
  94.5 0.1 reshape.70
  94.6 0.1 slice_reduce_fusion
  94.7 0.1 fusion.13
  94.8 8.1 %fusion.1 = f32[1024,720]{0,1:T(8,128)S(1)} fusion(bf16[1024,2880]{1,0:T(8,128)(2,1)} %all-gather.4.cloned.1.call-done, bf16[1,2880,720]{1,2,0:T(8,128)(2,1)} %param.14), kind=kOutput, calls=%fused_computation.2 | convolution fusion | flops 4246732800 | bytes 12994560 | tf_op jit(solution)/shard_map/dot_general | solution.py:43
  102.9 16.3 %convolution_convert_fusion = bf16[1024,2880]{0,1:T(8,128)(2,1)} fusion(bf16[1,720,2880]{2,1,0:T(8,128)(2,1)} %param.15, f32[1024,720]{0,1:T(8,128)S(1)} %fusion.1, bf16[1024,2880]{1,0:T(8,128)(2,1)} %all-gather.4.cloned.1.call-done, bf16[1,2880,720]{1,2,0:T(8,128)(2,1)} %param.13, f32[1024]{0:T(1024)S(1)} %fusion.13), kind=kOutput, calls=%fused_computation | convolution fusion | flops 8503050240 | bytes 23044096 | tf_op jit(solution)/shard_map/dot_general | solution.py:46
  119.1 0.0 reduce-scatter.5.cloned.1.call-update
  119.2 0.0 reduce-scatter.7.cloned.1.call-start
  119.2 64.1 %reduce-scatter.5.cloned.1.call-done = bf16[256,2880]{0,1:T(8,128)(2,1)} async-done(((bf16[1024,2880]{0,1:T(8,128)(2,1)}), bf16[256,2880]{0,1:T(8,128)(2,1)}) %reduce-scatter.5.cloned.1.call-update) | async-done | bytes 1474576 | tf_op jit(solution)/shard_map/reduce_scatter | solution.py:47
  183.3 2.6 %copy.12 = bf16[256,2880]{1,0:T(8,128)(2,1)} copy(bf16[256,2880]{0,1:T(8,128)(2,1)} %reduce-scatter.5.cloned.1.call-done) | data formatting | bytes 2949120
  185.9 0.0 reduce-scatter.7.cloned.1.call-update
  185.9 34.3 %reduce-scatter.7.cloned.1.call-done = bf16[32,2880]{1,0:T(8,128)(2,1)} async-done(((bf16[256,2880]{1,0:T(8,128)(2,1)}), bf16[32,2880]{1,0:T(8,128)(2,1)}) %reduce-scatter.7.cloned.1.call-update) | async-done | bytes 184336 | tf_op jit(solution)/shard_map/reduce_scatter | solution.py:48
  (3 shorter events, 0.0 us)
Async XLA Ops:
  6.5 88.2 %all-gather.4.cloned.1.call-start = ((), (), s32[]{:S(2)}) async-start(), calls=%async_computation.2 | async-start | bytes 6217728 | tf_op jit(solution)/shard_map/all_gather | solution.py:40
  7.3 176.0 %reduce-scatter.5.cloned.1.call-start = ((), (), s32[]{:S(2)}) async-start(), calls=%async_computation.3 | async-start | bytes 7372800 | tf_op jit(solution)/shard_map/reduce_scatter | solution.py:47
  119.2 101.0 %reduce-scatter.7.cloned.1.call-start = ((), (), s32[]{:S(2)}) async-start(), calls=%async_computation.4 | async-start | bytes 1695744 | tf_op jit(solution)/shard_map/reduce_scatter | solution.py:48
Sparse Core Ops, SparseCore 0:
  10.2 70.8 all-gather.3
  119.3 63.9 reduce-scatter.4
  186.0 34.1 reduce-scatter.6
where the time goes:
time: 227 us
  waiting for transfers between devices  99.1 us (44%)
  blocking collectives  82 us (36%)
  matrix products  24.4 us (11%)
  between operations  14.4 us (6%)
  other arithmetic  3.78 us (2%)
  local copies, waits for them, and re-layouts  2.97 us (1%)
    reduce_scatter x1, waiting for transfers between devices, on_device(): share = lax.psum_scatter(share, 'attn', scatter_dimension=0, tiled=True)  64.1 us
    all_gather x1, blocking collectives, on_device(): all_ids = lax.all_gather(expert_ids, both, axis=0, tiled=True)  44.1 us
    all_gather x1, blocking collectives, on_device(): all_probs = lax.all_gather(gate_probs, both, axis=0, tiled=True)  37.9 us
    reduce_scatter x1, waiting for transfers between devices, on_device(): return lax.psum_scatter(share, 'expert', scatter_dimension=0, tiled=True)  34.3 us
    dot_general x1, matrix products, on_device(): jnp.dot(hidden, down_weight[0], preferred_element_type=jnp.float32)  16.3 us
    dot_general x1, matrix products, on_device(): up_part = jnp.dot(rows, up_weight[0], preferred_element_type=jnp.float32)  8.09 us
  transfers between devices with their start and end apart: 3, of which 2 were waited for; matrix products, arithmetic and copies ran while one was open for 2% of the time, Pallas kernels for 0%

commit v1 on v0

--- a/solution.py
+++ b/solution.py
@@ -35,8 +35,16 @@
     capacity = tok_rows * top_count * lax.axis_size("attn")
     block_size = capacity // 8
     both = ("attn", "expert")
-    all_ids = lax.all_gather(expert_ids, both, axis=0, tiled=True)
-    all_probs = lax.all_gather(gate_probs, both, axis=0, tiled=True)
+
+    def serve_waves(field, inner_x):
+        state_now = jnp.split(
+            jax.lax.all_gather(jnp.concatenate([inner_x, field], axis=1), both, axis=0, tiled=True),
+            [inner_x.shape[1]],
+            axis=1,
+        )
+        return state_now
+
+    all_ids, all_probs = serve_waves(gate_probs, expert_ids)
     rows = lax.all_gather(tokens, both, axis=0, tiled=True)
     weight = row_weights(all_ids, all_probs, shed_blocks, partner, capacity, block_size)
     gate_part = jnp.dot(rows, gate_weight[0], preferred_element_type=jnp.float32)

time: 227 us -> 215 us (0.947)
  blocking collectives: 82 us -> 44 us
  waiting for transfers between devices: 99.1 us -> 124 us
    all_gather x2 -> x1, blocking collectives: 82 us -> 44 us  [serve_waves(): jax.lax.all_gather(jnp.concatenate([inner_x, field], axis=1), both, axis=...]
    all_gather x1, waiting for transfers between devices: 0.01 us -> 23.5 us  [on_device(): rows = lax.all_gather(tokens, both, axis=0, tiled=True)]
  transfers between devices with their start and end apart: 3 -> 3, of which waited for: 2 -> 3; matrix products, arithmetic and copies ran while one was open for 2% -> 3% of each run, Pallas kernels for 0% -> 0%
where the time goes in v1:
time: 215 us
  waiting for transfers between devices  124 us (58%)
  blocking collectives  44 us (20%)
  matrix products  24.4 us (11%)
  between operations  14.4 us (7%)
  other arithmetic  5.07 us (2%)
  local copies, waits for them, and re-layouts  2.89 us (1%)
    reduce_scatter x1, waiting for transfers between devices, on_device(): share = lax.psum_scatter(share, 'attn', scatter_dimension=0, tiled=True)  65.6 us
    all_gather x1, blocking collectives, serve_waves(): jax.lax.all_gather(jnp.concatenate([inner_x, field], axis=1), both, axis=...  44 us
    reduce_scatter x1, waiting for transfers between devices, on_device(): return lax.psum_scatter(share, 'expert', scatter_dimension=0, tiled=True)  34.3 us
    all_gather x1, waiting for transfers between devices, on_device(): rows = lax.all_gather(tokens, both, axis=0, tiled=True)  23.5 us
    dot_general x1, matrix products, on_device(): jnp.dot(hidden, down_weight[0], preferred_element_type=jnp.float32)  16.3 us
    dot_general x1, matrix products, on_device(): up_part = jnp.dot(rows, up_weight[0], preferred_element_type=jnp.float32)  8.09 us
  transfers between devices with their start and end apart: 3, of which 3 were waited for; matrix products, arithmetic and copies ran while one was open for 3% of the time, Pallas kernels for 0%

profile of v1, /device:TPU:0, one launch (start us, length us, event | category | flops | bytes accessed | tf_op | source)
XLA Modules:
  0.0 214.8 jit_solution(14172072868669368088)
XLA Ops:
  6.5 0.0 all-gather.3.cloned.1.call-start
  6.5 0.7 all-gather.3.cloned.1.call-update
  7.3 0.0 reduce-scatter.5.cloned.1.call-start
  7.3 1.3 fusion.15
  8.6 2.0 fusion.16
  11.8 0.7 convert_element_type.25
  12.5 0.7 maximum_bitcast_fusion
  13.2 44.0 %all-gather = f32[32,32,8]{1,2,0:T(8,128)S(1)} all-gather(f32[1,32,8]{1,2,0:T(8,128)S(1)} %maximum_bitcast_fusion), channel_id=1, replica_groups=mesh['attn'=4,'expert'=8] {'attn','expert'}, dimensions={0}, use_global_device_ids=true | all-gather | bytes 33792 | tf_op jit(solution)/shard_map/all_gather | solution.py:41
  57.2 0.1 reshape.60
  57.4 0.3 reduce-window.9
  57.6 0.1 slice.7
  57.7 0.1 slice_reduce_fusion
  57.9 0.1 fusion.14
  58.0 23.5 %all-gather.3.cloned.1.call-done = bf16[1024,2880]{1,0:T(8,128)(2,1)} async-done(((bf16[32,2880]{1,0:T(8,128)(2,1)}), bf16[1024,2880]{1,0:T(8,128)(2,1)}) %all-gather.3.cloned.1.call-update) | async-done | bytes 5898256 | tf_op jit(solution)/shard_map/all_gather | solution.py:48
  81.4 8.1 %fusion.1 = f32[1024,720]{0,1:T(8,128)S(1)} fusion(bf16[1024,2880]{1,0:T(8,128)(2,1)} %all-gather.3.cloned.1.call-done, bf16[1,2880,720]{1,2,0:T(8,128)(2,1)} %param.14), kind=kOutput, calls=%fused_computation.2 | convolution fusion | flops 4246732800 | bytes 12994560 | tf_op jit(solution)/shard_map/dot_general | solution.py:51
  89.5 16.3 %convolution_convert_fusion = bf16[1024,2880]{0,1:T(8,128)(2,1)} fusion(bf16[1,720,2880]{2,1,0:T(8,128)(2,1)} %param.15, f32[1024,720]{0,1:T(8,128)S(1)} %fusion.1, bf16[1024,2880]{1,0:T(8,128)(2,1)} %all-gather.3.cloned.1.call-done, bf16[1,2880,720]{1,2,0:T(8,128)(2,1)} %param.13, f32[1024]{0:T(1024)S(1)} %fusion.14), kind=kOutput, calls=%fused_computation | convolution fusion | flops 8503050240 | bytes 23044096 | tf_op jit(solution)/shard_map/dot_general | solution.py:54
  105.8 0.0 reduce-scatter.5.cloned.1.call-update
  105.8 0.0 reduce-scatter.7.cloned.1.call-start
  105.9 65.6 %reduce-scatter.5.cloned.1.call-done = bf16[256,2880]{0,1:T(8,128)(2,1)} async-done(((bf16[1024,2880]{0,1:T(8,128)(2,1)}), bf16[256,2880]{0,1:T(8,128)(2,1)}) %reduce-scatter.5.cloned.1.call-update) | async-done | bytes 1474576 | tf_op jit(solution)/shard_map/reduce_scatter | solution.py:55
  171.4 2.6 %copy.14 = bf16[256,2880]{1,0:T(8,128)(2,1)} copy(bf16[256,2880]{0,1:T(8,128)(2,1)} %reduce-scatter.5.cloned.1.call-done) | data formatting | bytes 2949120
  174.0 0.0 reduce-scatter.7.cloned.1.call-update
  174.0 34.3 %reduce-scatter.7.cloned.1.call-done = bf16[32,2880]{1,0:T(8,128)(2,1)} async-done(((bf16[256,2880]{1,0:T(8,128)(2,1)}), bf16[32,2880]{1,0:T(8,128)(2,1)}) %reduce-scatter.7.cloned.1.call-update) | async-done | bytes 184336 | tf_op jit(solution)/shard_map/reduce_scatter | solution.py:56
  (5 shorter events, 0.1 us)
Async XLA Ops:
  6.5 74.9 %all-gather.3.cloned.1.call-start = ((), (), s32[]{:S(2)}) async-start(), calls=%async_computation.2 | async-start | bytes 6217728 | tf_op jit(solution)/shard_map/all_gather | solution.py:48
  7.3 164.2 %reduce-scatter.5.cloned.1.call-start = ((), (), s32[]{:S(2)}) async-start(), calls=%async_computation.3 | async-start | bytes 7372800 | tf_op jit(solution)/shard_map/reduce_scatter | solution.py:55
  105.8 102.5 %reduce-scatter.7.cloned.1.call-start = ((), (), s32[]{:S(2)}) async-start(), calls=%async_computation.4 | async-start | bytes 1695744 | tf_op jit(solution)/shard_map/reduce_scatter | solution.py:56
Sparse Core Ops, SparseCore 0:
  10.2 71.2 all-gather.2
  106.0 65.4 reduce-scatter.4
  174.2 34.1 reduce-scatter.6
